TPU v7x, 32 devices: a whole 2x2x4 slice. The times are simulated.
32 devices in a mesh: wide: 8 (over y, x, core), narrow: 4 (over z).
Axes of the slice: x: 2, y: 2, z: 4, core: 2. Of those that a mesh axis runs over, the one named last changes fastest.
Arguments:
- coefficients: float32 [8, 8192, 8192], P(None, 'wide', 'narrow'), may hold values from -0.07 to 0.07
- tensor_blocks: float32 [8, 32, 8192], P(None, 'wide', 'narrow'), may hold values from -6 to 6
- basis_rows: float32 [32, 8192], P(None, ('wide', 'narrow')), may hold values from -1.1 to 1.1, as said below
Outputs:
- new_basis: float32 [32, 8192], P(None, ('wide', 'narrow'))
- projection: float32 [32, 32], replicated
- factor: float32 [32, 32], replicated
Inputs may be any that keep to these rules, and one draw needn't show every extreme that they name: The rows of basis_rows are nearly but not exactly orthonormal: basis_rows basis_rows^T differs from the identity by less than 0.2 in spectral norm.
All inputs are finite; a program needn't handle non-finite values.
Results may differ from a plain program's by a relative error of at most 0.0002.
Values sent between devices are 32-bit elements; how exact they have to be, the bound alone decides.
A program may use at most 128 MiB of HBM per device.

v0:
```python
import jax
import jax.numpy as jnp
from jax import lax
from jax.sharding import PartitionSpec as P

N = 8192


def body(coefficients, tensor_blocks, basis_rows):
    hi = lax.Precision.HIGHEST
    partial_block = jnp.einsum(
        "kic,krc->ir",
        lax.all_gather(tensor_blocks, "wide", axis=1, tiled=True),
        coefficients,
        precision=hi,
    )
    image = lax.psum_scatter(partial_block, "narrow", scatter_dimension=1, tiled=True)
    local_first = jnp.dot(basis_rows, image.T, precision=hi)
    local_correlation = jnp.dot(basis_rows, basis_rows.T, precision=hi)
    first, correlation = lax.psum((local_first, local_correlation), ("wide", "narrow"))
    once = image - jnp.dot(first.T, basis_rows, precision=hi)
    second, raw_gram = lax.psum(
        (jnp.dot(basis_rows, once.T, precision=hi), jnp.dot(once, once.T, precision=hi)),
        ("wide", "narrow"),
    )
    twice = once - jnp.dot(second.T, basis_rows, precision=hi)
    cross = jnp.dot(second.T, second, precision=hi)
    weighted = jnp.dot(second.T, jnp.dot(correlation, second, precision=hi), precision=hi)
    gram = (raw_gram - 2.0 * cross + weighted) / N
    factor = jnp.linalg.cholesky(gram)
    new_basis = lax.linalg.triangular_solve(factor, twice, left_side=True, lower=True)
    return (new_basis, first + second, factor)


def solution(mesh):
    in_specs = (P(None, "wide", "narrow"), P(None, "wide", "narrow"), P(None, ("wide", "narrow")))
    out_specs = (P(None, ("wide", "narrow")), P(), P())
    return jax.shard_map(body, mesh=mesh, in_specs=in_specs, out_specs=out_specs, check_vma=False)
```

profile of v0, /device:TPU:0, one launch (start us, length us, event | category | flops | bytes accessed | tf_op | source)
XLA Modules:
  0.0 225.5 jit_solution(1987830653347588551)
XLA Ops:
  7.2 0.0 all-gather.2.cloned.1.call-start
  7.2 1.8 copy.11
  9.1 0.0 reduce-scatter.2.cloned.1.call-start
  9.1 31.3 %all-gather.2.cloned.1.call-done = f32[8,32,2048]{2,0,1:T(8,128)} async-done(((f32[8,4,2048]{2,0,1:T(8,128)}), f32[8,32,2048]{2,0,1:T(8,128)}) %all-gather.2.cloned.1.call-update) | async-done | bytes 2097168 | tf_op jit(solution)/shard_map/all_gather | solution.py:13
  40.4 67.1 %fusion.2 = f32[32,1024]{1,0:T(8,128)} fusion(f32[8,1024,2048]{2,1,0:T(8,128)} %param.3, f32[8,32,2048]{2,0,1:T(8,128)} %all-gather.2.cloned.1.call-done), kind=kOutput, calls=%fused_computation.2 | convolution fusion | flops 6442450944 | bytes 69337088 | tf_op jit(solution)/shard_map/kic,krc->ir/dot_general | solution.py:11
  107.5 0.2 fusion.11
  107.7 19.4 %reduce-scatter.2.cloned.1.call-done = f32[32,256]{1,0:T(8,128)} async-done(((f32[32,1024]{1,0:T(8,128)}), f32[32,256]{1,0:T(8,128)}) %reduce-scatter.2.cloned.1.call-update) | async-done | bytes 32784 | tf_op jit(solution)/shard_map/reduce_scatter | solution.py:17
  127.1 0.9 convolution_bitcast_fusion.1
  128.1 38.5 %psum.28 = f32[32,32]{0,1:T(8,128)S(1)} all-reduce(f32[32,32]{0,1:T(8,128)S(1)} %convolution_bitcast_fusion.1), channel_id=1, replica_groups=mesh['wide'=8,'narrow'=4] {'wide','narrow'}, use_global_device_ids=true, to_apply=%region_1.0 | all-reduce | flops 1024 | bytes 8192 | tf_op jit(solution)/shard_map/psum | solution.py:20
  166.5 0.9 convolution_subtract_fusion.1
  167.4 0.2 convolution_bitcast_fusion
  167.6 0.2 fusion.10
  167.8 41.3 %all-reduce = (f32[32,32]{0,1:T(8,128)S(1)}, f32[32,32]{0,1:T(8,128)S(1)}, f32[32,32]{1,0:T(8,128)S(1)}) all-reduce(f32[32,32]{0,1:T(8,128)S(1)} %convolution_bitcast_fusion, f32[32,32]{0,1:T(8,128)S(1)} %fusion.10, f32[32,32]{1,0:T(8,128)S(1)} %fusion.11), channel_id=1, replica_groups=mesh['wide'=8,'narrow'=4] {'wide','narrow'}, use_global_device_ids=true, to_apply=%region_3.0 | all-reduce | flops 3072 | bytes 24576 | tf_op jit(solution)/shard_map/psum | solution.py:22
  209.1 0.2 convolution_subtract_fusion
  209.2 0.1 fusion.12
  209.4 0.2 fusion.6
  209.6 0.2 fusion.5
  209.8 0.1 copy.16
  209.9 2.9 %cholesky.16 = f32[32,32]{1,0:T(8,128)S(1)} custom-call(f32[32,32]{1,0:T(8,128)S(1)} %fusion.9), custom_call_target="Cholesky" | custom-call | tf_op jit(solution)/shard_map/jit(cholesky)/cholesky | solution.py:30
  212.8 0.6 compare_reduce_fusion
  213.5 1.3 select_bitcast_fusion
  214.7 2.4 %custom-call.6 = f32[1,32,32]{1,2,0:T(8,128)S(1)} custom-call(f32[1,32,32]{2,1,0:T(8,128)S(1)} %get-tuple-element.12), custom_call_target="InvertDiagBlocksLowerTriangular" | custom-call | tf_op jit(solution)/shard_map/triangular_solve | solution.py:31
  217.1 0.7 copy.17
  217.9 0.8 fusion.7
  (7 shorter events, 0.1 us)
Async XLA Ops:
  7.2 100.4 %copy-start = (f32[32,256]{1,0:T(8,128)S(1)}, f32[32,256]{1,0:T(8,128)}, u32[]{:S(2)}) copy-start(f32[32,256]{1,0:T(8,128)} %param.5) | copy-start | bytes 98308
  7.2 33.2 %all-gather.2.cloned.1.call-start = ((), (), s32[]{:S(2)}) async-start(), calls=%async_computation.1 | async-start | bytes 2359296 | tf_op jit(solution)/shard_map/all_gather | solution.py:13
  9.1 118.1 %reduce-scatter.2.cloned.1.call-start = ((), (), s32[]{:S(2)}) async-start(), calls=%async_computation.2 | async-start | bytes 163840 | tf_op jit(solution)/shard_map/reduce_scatter | solution.py:17
Sparse Core Ops, SparseCore 0:
  9.9 30.4 all-gather.1
  107.7 19.4 reduce-scatter.1
where the time goes:
time: 226 us
  blocking collectives  79.7 us (35%)
  matrix products  70.9 us (31%)
  waiting for transfers between devices  50.7 us (22%)
  between operations  14.1 us (6%)
  other arithmetic  7.3 us (3%)
  local copies, waits for them, and re-layouts  2.62 us (1%)
    dot_general x1, matrix products, body(): jnp.einsum('kic,krc->ir', lax.all_gather(tensor_blocks, 'wide', axis=1, t...  67.1 us
    psum x1, blocking collectives, body(): lax.psum((jnp.dot(basis_rows, once.T, precision=hi), jnp.dot(once, once.T...  41.3 us
    psum x1, blocking collectives, body(): lax.psum((local_first, local_correlation), ('wide', 'narrow'))  38.5 us
    all_gather x1, waiting for transfers between devices, body(): lax.all_gather(tensor_blocks, 'wide', axis=1, tiled=True)  31.3 us
    reduce_scatter x1, waiting for transfers between devices, body(): lax.psum_scatter(partial_block, 'narrow', scatter_dimension=1, tiled=True)  19.4 us
  transfers between devices with their start and end apart: 2, of which 2 were waited for; matrix products, arithmetic and copies ran while one was open for 0% of the time, Pallas kernels for 0%

commit v1 on v0

--- a/solution.py
+++ b/solution.py
@@ -6,13 +6,23 @@
 N = 8192
 
 
+def collect(x, axis, dim):
+    ways = lax.axis_size(axis)
+    up = [(d, (d + 1) % ways) for d in range(ways)]
+    down = [(d, (d - 1) % ways) for d in range(ways)]
+    earlier, later = ([x], [x])
+    for _ in range(ways // 2):
+        earlier.append(lax.ppermute(earlier[-1], axis, up))
+    for _ in range((ways - 1) // 2):
+        later.append(lax.ppermute(later[-1], axis, down))
+    line = jnp.concatenate([*earlier[::-1], *later[1:]], axis=dim)
+    return jnp.roll(line, (lax.axis_index(axis) - ways // 2) * x.shape[dim], axis=dim)
+
+
 def body(coefficients, tensor_blocks, basis_rows):
     hi = lax.Precision.HIGHEST
     partial_block = jnp.einsum(
-        "kic,krc->ir",
-        lax.all_gather(tensor_blocks, "wide", axis=1, tiled=True),
-        coefficients,
-        precision=hi,
+        "kic,krc->ir", collect(tensor_blocks, "wide", 1), coefficients, precision=hi
     )
     image = lax.psum_scatter(partial_block, "narrow", scatter_dimension=1, tiled=True)
     local_first = jnp.dot(basis_rows, image.T, precision=hi)

time: 226 us -> 237 us (1.049)
  starting transfers between devices: 0.08 us -> 9.96 us
  local copies, waits for them, and re-layouts: 2.62 us -> 10 us
  waiting for transfers between devices: 50.7 us -> 44.9 us
    all_gather x1 -> x0, waiting for transfers between devices: 31.3 us -> none  [body(): lax.all_gather(tensor_blocks, 'wide', axis=1, tiled=True)]
    ppermute x0 -> x7, waiting for transfers between devices: none -> 19.1 us  [the longest x4 15.1 us: collect(): earlier.append(lax.ppermute(earlier[-1], axis, up))]
    ppermute x0 -> x7, starting transfers between devices: none -> 9.92 us  [the longest x3 8.44 us: collect(): later.append(lax.ppermute(later[-1], axis, down))]
    concatenate x0 -> x1, local copies, waits for them, and re-layouts: none -> 9.22 us  [collect(): jnp.roll(line, (lax.axis_index(axis) - ways // 2) * x.shape[dim], axis=dim)]
    reduce_scatter x1, waiting for transfers between devices: 19.4 us -> 25.8 us  [body(): lax.psum_scatter(partial_block, 'narrow', scatter_dimension=1, tiled=True)]
  transfers between devices with their start and end apart: 2 -> 8, of which waited for: 2 -> 8; matrix products, arithmetic and copies ran while one was open for 0% -> 0% of each run, Pallas kernels for 0% -> 0%
where the time goes in v1:
time: 237 us
  blocking collectives  80 us (34%)
  matrix products  70.6 us (30%)
  waiting for transfers between devices  44.9 us (19%)
  between operations  14.1 us (6%)
  local copies, waits for them, and re-layouts  10 us (4%)
  starting transfers between devices  9.96 us (4%)
  other arithmetic  7.3 us (3%)
    dot_general x1, matrix products, body(): jnp.einsum('kic,krc->ir', collect(tensor_blocks, 'wide', 1), coefficients...  66.8 us
    psum x1, blocking collectives, body(): lax.psum((jnp.dot(basis_rows, once.T, precision=hi), jnp.dot(once, once.T...  41.3 us
    psum x1, blocking collectives, body(): lax.psum((local_first, local_correlation), ('wide', 'narrow'))  38.6 us
    reduce_scatter x1, waiting for transfers between devices, body(): lax.psum_scatter(partial_block, 'narrow', scatter_dimension=1, tiled=True)  25.8 us
    ppermute x4, waiting for transfers between devices, collect(): earlier.append(lax.ppermute(earlier[-1], axis, up))  15.1 us
    concatenate x1, local copies, waits for them, and re-layouts, collect(): jnp.roll(line, (lax.axis_index(axis) - ways // 2) * x.shape[dim], axis=dim)  9.22 us
    ppermute x3, starting transfers between devices, collect(): later.append(lax.ppermute(later[-1], axis, down))  8.44 us
  transfers between devices with their start and end apart: 8, of which 8 were waited for; matrix products, arithmetic and copies ran while one was open for 0% of the time, Pallas kernels for 0%

profile of v1, /device:TPU:0, one launch (start us, length us, event | category | flops | bytes accessed | tf_op | source)
XLA Modules:
  0.0 236.9 jit_solution(6023004339259775692)
XLA Ops:
  7.8 2.9 %collective-permute-start.4 = (f32[8,4,2048]{2,1,0:T(4,128)}, f32[8,4,2048]{2,1,0:T(4,128)S(1)}, u32[]{:S(2)}, u32[]{:S(2)}) collective-permute-start(f32[8,4,2048]{2,1,0:T(4,128)} %param.4), channel_id=1, source_target_pairs={{0,28},{4,0},{8,4},{12,8},{16,12},{20,16},{24,20},{28,24},{1,29},{... | collective-permute-start | bytes 786440 | tf_op jit(solution)/shard_map/ppermute | solution.py:17
  10.7 4.4 %collective-permute-done = f32[8,4,2048]{2,1,0:T(4,128)S(1)} collective-permute-done((f32[8,4,2048]{2,1,0:T(4,128)}, f32[8,4,2048]{2,1,0:T(4,128)S(1)}, u32[]{:S(2)}, u32[]{:S(2)}) %collective-permute-start) | collective-permute-done | bytes 262176 | tf_op jit(solution)/shard_map/ppermute | solution.py:15
  15.1 0.6 collective-permute-start.1
  15.8 0.9 collective-permute-done.4
  16.7 2.7 %collective-permute-start.5 = (f32[8,4,2048]{2,1,0:T(4,128)S(1)}, f32[8,4,2048]{2,1,0:T(4,128)S(1)}, u32[]{:S(2)}, u32[]{:S(2)}) collective-permute-start(f32[8,4,2048]{2,1,0:T(4,128)S(1)} %collective-permute-done.4), channel_id=1, source_target_pairs={{0,28},{4,0},{8,4},{12,8},{16,12},{20,16},{24,20},{28,24},{1,29},{... | collective-permute-start | bytes 786440 | tf_op jit(solution)/shard_map/ppermute | solution.py:17
  19.4 2.7 %collective-permute-done.1 = f32[8,4,2048]{2,1,0:T(4,128)S(1)} collective-permute-done((f32[8,4,2048]{2,1,0:T(4,128)S(1)}, f32[8,4,2048]{2,1,0:T(4,128)S(1)}, u32[]{:S(2)}, u32[]{:S(2)}) %collective-permute-start.1) | collective-permute-done | bytes 262176 | tf_op jit(solution)/shard_map/ppermute | solution.py:15
  22.3 1.8 collective-permute-done.5
  24.1 2.8 %collective-permute-start.6 = (f32[8,4,2048]{2,1,0:T(4,128)S(1)}, f32[8,4,2048]{2,1,0:T(4,128)S(1)}, u32[]{:S(2)}, u32[]{:S(2)}) collective-permute-start(f32[8,4,2048]{2,1,0:T(4,128)S(1)} %collective-permute-done.5), channel_id=1, source_target_pairs={{0,28},{4,0},{8,4},{12,8},{16,12},{20,16},{24,20},{28,24},{1,29},{... | collective-permute-start | bytes 786440 | tf_op jit(solution)/shard_map/ppermute | solution.py:17
  27.0 2.6 %collective-permute-done.2 = f32[8,4,2048]{2,1,0:T(4,128)S(1)} collective-permute-done((f32[8,4,2048]{2,1,0:T(4,128)S(1)}, f32[8,4,2048]{2,1,0:T(4,128)S(1)}, u32[]{:S(2)}, u32[]{:S(2)}) %collective-permute-start.2) | collective-permute-done | bytes 262176 | tf_op jit(solution)/shard_map/ppermute | solution.py:15
  29.6 1.3 collective-permute-done.6
  30.8 5.4 %collective-permute-done.3 = f32[8,4,2048]{2,1,0:T(4,128)S(1)} collective-permute-done((f32[8,4,2048]{2,1,0:T(4,128)S(1)}, f32[8,4,2048]{2,1,0:T(4,128)S(1)}, u32[]{:S(2)}, u32[]{:S(2)}) %collective-permute-start.3) | collective-permute-done | bytes 262176 | tf_op jit(solution)/shard_map/ppermute | solution.py:15
  36.3 9.2 %concatenate.6 = f32[8,64,2048]{2,1,0:T(8,128)} concatenate(f32[8,4,2048]{2,1,0:T(4,128)S(1)} %collective-permute-done.3, f32[8,4,2048]{2,1,0:T(4,128)S(1)} %collective-permute-done.2, f32[8,4,2048]{2,1,0:T(4,128)S(1)} %collective-permute-done.1, f32[8,4,2048]{2,1,0:T(4,128)S(1)} %collective-permute-done, f32[8,4,2048]{2,1,0:T(4,128)} %param.4, ...), dimensions={1} | concatenate | bytes 8388608 | tf_op jit(solution)/shard_map/jit(_roll_dynamic)/concatenate | solution.py:19
  45.5 66.8 %fusion.2 = f32[32,1024]{1,0:T(8,128)} fusion(f32[8,1024,2048]{2,1,0:T(8,128)} %param.3, f32[8,64,2048]{2,1,0:T(8,128)} %concatenate.6, s32[]{:T(128)S(6)} %select_n.18), kind=kOutput, calls=%fused_computation.2 | convolution fusion | flops 6442450944 | bytes 69337088 | tf_op jit(solution)/shard_map/kic,krc->ir/dot_general | solution.py:24
  112.5 25.8 %reduce-scatter.2.cloned.1.call-done = f32[32,256]{1,0:T(8,128)} async-done(((f32[32,1024]{1,0:T(8,128)}), f32[32,256]{1,0:T(8,128)}) %reduce-scatter.2.cloned.1.call-update) | async-done | bytes 32784 | tf_op jit(solution)/shard_map/reduce_scatter | solution.py:27
  138.3 0.9 convolution_bitcast_fusion.1
  139.2 38.6 %psum.28 = f32[32,32]{0,1:T(8,128)S(1)} all-reduce(f32[32,32]{0,1:T(8,128)S(1)} %convolution_bitcast_fusion.1), channel_id=1, replica_groups=mesh['wide'=8,'narrow'=4] {'wide','narrow'}, use_global_device_ids=true, to_apply=%region_1.2 | all-reduce | flops 1024 | bytes 8192 | tf_op jit(solution)/shard_map/psum | solution.py:30
  177.8 0.9 convolution_subtract_fusion.1
  179.1 41.3 %all-reduce = (f32[32,32]{0,1:T(8,128)S(1)}, f32[32,32]{0,1:T(8,128)S(1)}, f32[32,32]{1,0:T(8,128)S(1)}) all-reduce(f32[32,32]{0,1:T(8,128)S(1)} %convolution_bitcast_fusion, f32[32,32]{0,1:T(8,128)S(1)} %fusion.11, f32[32,32]{1,0:T(8,128)S(1)} %fusion.12), channel_id=1, replica_groups=mesh['wide'=8,'narrow'=4] {'wide','narrow'}, use_global_device_ids=true, to_apply=%region_3.4 | all-reduce | flops 3072 | bytes 24576 | tf_op jit(solution)/shard_map/psum | solution.py:32
  221.2 2.9 %cholesky.16 = f32[32,32]{1,0:T(8,128)S(1)} custom-call(f32[32,32]{1,0:T(8,128)S(1)} %fusion.9), custom_call_target="Cholesky" | custom-call | tf_op jit(solution)/shard_map/jit(cholesky)/cholesky | solution.py:40
  224.2 0.6 compare_reduce_fusion
  224.8 1.3 select_bitcast_fusion
  226.1 2.4 %custom-call.6 = f32[1,32,32]{1,2,0:T(8,128)S(1)} custom-call(f32[1,32,32]{2,1,0:T(8,128)S(1)} %get-tuple-element.9), custom_call_target="InvertDiagBlocksLowerTriangular" | custom-call | tf_op jit(solution)/shard_map/triangular_solve | solution.py:41
  228.5 0.7 copy.10
  229.2 0.8 fusion.7
  (18 shorter events, 2.2 us)
Async XLA Ops:
  7.2 105.2 %copy-start = (f32[32,256]{1,0:T(8,128)S(1)}, f32[32,256]{1,0:T(8,128)}, u32[]{:S(2)}) copy-start(f32[32,256]{1,0:T(8,128)} %param.5) | copy-start | bytes 98308
  7.2 131.1 %reduce-scatter.2.cloned.1.call-start = ((), (), s32[]{:S(2)}) async-start(), calls=%async_computation.1 | async-start | bytes 163840 | tf_op jit(solution)/shard_map/reduce_scatter | solution.py:27
  7.2 7.9 %collective-permute-start = (f32[8,4,2048]{2,1,0:T(4,128)}, f32[8,4,2048]{2,1,0:T(4,128)S(1)}, u32[]{:S(2)}, u32[]{:S(2)}) collective-permute-start(f32[8,4,2048]{2,1,0:T(4,128)} %param.4), channel_id=1, source_target_pairs={{0,4},{4,8},{8,12},{12,16},{16,20},{20,24},{24,28},{28,0},{1,5},{5... | collective-permute-start | bytes 786440 | tf_op jit(solution)/shard_map/ppermute | solution.py:15
  7.8 8.9 %collective-permute-start.4 = (f32[8,4,2048]{2,1,0:T(4,128)}, f32[8,4,2048]{2,1,0:T(4,128)S(1)}, u32[]{:S(2)}, u32[]{:S(2)}) collective-permute-start(f32[8,4,2048]{2,1,0:T(4,128)} %param.4), channel_id=1, source_target_pairs={{0,28},{4,0},{8,4},{12,8},{16,12},{20,16},{24,20},{28,24},{1,29},{... | collective-permute-start | bytes 786440 | tf_op jit(solution)/shard_map/ppermute | solution.py:17
  15.1 6.9 %collective-permute-start.1 = (f32[8,4,2048]{2,1,0:T(4,128)S(1)}, f32[8,4,2048]{2,1,0:T(4,128)S(1)}, u32[]{:S(2)}, u32[]{:S(2)}) collective-permute-start(f32[8,4,2048]{2,1,0:T(4,128)S(1)} %collective-permute-done), channel_id=1, source_target_pairs={{0,4},{4,8},{8,12},{12,16},{16,20},{20,24},{24,28},{28,0},{1,5},{5... | collective-permute-start | bytes 786440 | tf_op jit(solution)/shard_map/ppermute | solution.py:15
  16.7 7.5 %collective-permute-start.5 = (f32[8,4,2048]{2,1,0:T(4,128)S(1)}, f32[8,4,2048]{2,1,0:T(4,128)S(1)}, u32[]{:S(2)}, u32[]{:S(2)}) collective-permute-start(f32[8,4,2048]{2,1,0:T(4,128)S(1)} %collective-permute-done.4), channel_id=1, source_target_pairs={{0,28},{4,0},{8,4},{12,8},{16,12},{20,16},{24,20},{28,24},{1,29},{... | collective-permute-start | bytes 786440 | tf_op jit(solution)/shard_map/ppermute | solution.py:17
  22.0 7.5 %collective-permute-start.2 = (f32[8,4,2048]{2,1,0:T(4,128)S(1)}, f32[8,4,2048]{2,1,0:T(4,128)S(1)}, u32[]{:S(2)}, u32[]{:S(2)}) collective-permute-start(f32[8,4,2048]{2,1,0:T(4,128)S(1)} %collective-permute-done.1), channel_id=1, source_target_pairs={{0,4},{4,8},{8,12},{12,16},{16,20},{20,24},{24,28},{28,0},{1,5},{5... | collective-permute-start | bytes 786440 | tf_op jit(solution)/shard_map/ppermute | solution.py:15
  24.1 6.7 %collective-permute-start.6 = (f32[8,4,2048]{2,1,0:T(4,128)S(1)}, f32[8,4,2048]{2,1,0:T(4,128)S(1)}, u32[]{:S(2)}, u32[]{:S(2)}) collective-permute-start(f32[8,4,2048]{2,1,0:T(4,128)S(1)} %collective-permute-done.5), channel_id=1, source_target_pairs={{0,28},{4,0},{8,4},{12,8},{16,12},{20,16},{24,20},{28,24},{1,29},{... | collective-permute-start | bytes 786440 | tf_op jit(solution)/shard_map/ppermute | solution.py:17
  29.6 6.7 %collective-permute-start.3 = (f32[8,4,2048]{2,1,0:T(4,128)S(1)}, f32[8,4,2048]{2,1,0:T(4,128)S(1)}, u32[]{:S(2)}, u32[]{:S(2)}) collective-permute-start(f32[8,4,2048]{2,1,0:T(4,128)S(1)} %collective-permute-done.2), channel_id=1, source_target_pairs={{0,4},{4,8},{8,12},{12,16},{16,20},{20,24},{24,28},{28,0},{1,5},{5... | collective-permute-start | bytes 786440 | tf_op jit(solution)/shard_map/ppermute | solution.py:15
Sparse Core Ops, SparseCore 0:
  112.5 25.7 reduce-scatter.1
